TPU v7x, 512 devices: a whole 4x8x8 slice. The times are simulated.
512 devices in a mesh: row: 16 (over y, core), col: 32 (over z, x).
Axes of the slice: x: 4, y: 8, z: 8, core: 2. Of those that a mesh axis runs over, the one named last changes fastest.
Arguments:
- templates: float32 [1536, 3, 1024], P(('row', 'col')), may hold values from -600 to 600
Outputs:
- similar: float32 [1536, 1536], P(('row', 'col'))
All inputs are finite; a program needn't handle non-finite values.
Results may differ from a plain program's by a relative error of at most 0.0012.
Values may be sent and summed in bfloat16 or wider, within the bound.
No kernel may reach another device: no remote copies, remote signals or barrier semaphores. Data moves between devices by JAX's collectives and lax.ppermute only.
A program may use at most 128 MiB of HBM per device.

v0:
```python
import math

import jax
import jax.numpy as jnp
from jax import lax
from jax.sharding import PartitionSpec as P

LAGS = 512


def copy_for_each(array, axis):
    copies = jnp.broadcast_to(array, (lax.axis_size(axis), *array.shape))
    return lax.all_to_all(copies, axis, split_axis=0, concat_axis=0, tiled=True)


def in_order(tiles, dim):
    shape = list(tiles.shape[1:])
    shape[dim] *= tiles.shape[0]
    return jnp.moveaxis(tiles, 0, dim).reshape(shape)


def collect(array, axis, dim):
    tiles = copy_for_each(array, axis)
    return in_order(tiles, dim)


def normalize(templates):
    scaling = lax.rsqrt(jnp.mean(templates * templates, axis=2, keepdims=True) + 1e-06) / math.sqrt(
        templates.shape[2]
    )
    return (templates * scaling).astype(jnp.bfloat16)


def forward_table(samples, transform_len):
    half_len = transform_len // 2
    sample_idx = jnp.arange(samples, dtype=jnp.int32)[:, None]
    slot_idx = jnp.arange(transform_len, dtype=jnp.int32)[None, :]
    freq_idx = jnp.where(slot_idx < half_len, slot_idx, slot_idx - half_len)
    phases = sample_idx * freq_idx % transform_len
    angles = phases.astype(jnp.float32) * (2.0 * math.pi / transform_len)
    nyquist = jnp.where(sample_idx % 2 == 0, 1.0, -1.0)
    basis = jnp.where(
        slot_idx < half_len,
        jnp.cos(angles),
        jnp.where(slot_idx == half_len, nyquist, -jnp.sin(angles)),
    )
    return basis.astype(jnp.bfloat16)


def inverse_table(transform_len, lag_total):
    half_len = transform_len // 2
    slot_idx = jnp.arange(transform_len, dtype=jnp.int32)[:, None]
    lag_idx = jnp.arange(lag_total, dtype=jnp.int32)[None, :] - lag_total // 2
    freq_idx = jnp.where(slot_idx < half_len, slot_idx, slot_idx - half_len)
    phases = freq_idx * lag_idx % transform_len
    angles = phases.astype(jnp.float32) * (2.0 * math.pi / transform_len)
    weight = jnp.where(freq_idx == 0, 1.0, 2.0) / transform_len
    nyquist = jnp.where(lag_idx % 2 == 0, 1.0, -1.0) / transform_len
    basis = jnp.where(
        slot_idx < half_len,
        weight * jnp.cos(angles),
        jnp.where(slot_idx == half_len, nyquist, -weight * jnp.sin(angles)),
    )
    return basis.astype(jnp.bfloat16)


def spectra_of(normed, basis):
    row_total, comps, samples = normed.shape
    flattened = normed.reshape(row_total * comps, samples)
    spectrum = jnp.dot(flattened, basis, preferred_element_type=jnp.float32)
    return spectrum.astype(jnp.bfloat16).reshape(row_total, comps, basis.shape[1])


def pair_einsum(left_part, right_part):
    return jnp.einsum("icf,jcf->ijf", left_part.astype(jnp.float32), right_part.astype(jnp.float32))


def similarity(left_spec, right_spec, inverse):
    half_len = left_spec.shape[2] // 2
    left_real = left_spec[:, :, :half_len]
    left_imag = left_spec[:, :, half_len:]
    right_real = right_spec[:, :, :half_len]
    right_imag = right_spec[:, :, half_len:]
    above_zero = jnp.arange(half_len, dtype=jnp.int32) >= 1
    right_masked = jnp.where(above_zero, right_imag, jnp.zeros_like(right_imag))
    left_masked = jnp.where(above_zero, left_real, jnp.zeros_like(left_real))
    right_turned = jnp.where(above_zero, -right_real, right_imag)
    even_part = pair_einsum(
        jnp.concatenate([left_real, left_imag], axis=1),
        jnp.concatenate([right_real, right_masked], axis=1),
    )
    odd_part = pair_einsum(
        jnp.concatenate([left_masked, left_imag], axis=1),
        jnp.concatenate([right_imag, right_turned], axis=1),
    )
    cross_spec = jnp.concatenate([even_part, odd_part], axis=2).astype(jnp.bfloat16)
    left_rows = left_spec.shape[0]
    right_rows = right_spec.shape[0]
    lagged = jnp.dot(
        cross_spec.reshape(left_rows * right_rows, 2 * half_len),
        inverse,
        preferred_element_type=jnp.float32,
    )
    return jnp.max(lagged, axis=1).reshape(left_rows, right_rows)


def body(templates):
    per_device = templates.shape[0]
    samples = templates.shape[2]
    transform_len = samples + LAGS // 2
    forward = forward_table(samples, transform_len)
    inverse = inverse_table(transform_len, LAGS)
    local_waves = normalize(templates)
    outgoing = spectra_of(local_waves, forward)
    row_count = lax.axis_size("row")
    col_count = lax.axis_size("col")
    partners = collect(outgoing, "row", 0)
    pair_block = similarity(collect(outgoing, "col", 0), partners, inverse)
    owned_rows = lax.all_to_all(pair_block, "col", split_axis=0, concat_axis=1, tiled=True)
    reordered = owned_rows.reshape(per_device, col_count, row_count, per_device).transpose(
        0, 2, 1, 3
    )
    return reordered.reshape(per_device, col_count * row_count * per_device)


def solution(mesh):
    placed = (P(("row", "col"), None, None),)
    return jax.shard_map(
        body, mesh=mesh, in_specs=placed, out_specs=P(("row", "col"), None), check_vma=False
    )
```

profile of v0, /device:TPU:1, one launch (start us, length us, event | category | flops | bytes accessed | tf_op | source)
XLA Modules:
  0.0 158.0 jit_solution(2501880423134903222)
XLA Ops:
  0.0 0.9 multiply_reduce_fusion
  0.9 0.9 multiply_convert_fusion
  1.8 22.6 %fusion.20 = bf16[9,1280]{1,0:T(8,128)(2,1)S(1)} fusion(bf16[9,1024]{1,0:T(8,128)(2,1)S(1)} %reshape.135, bf16[1024]{0:T(1024)(128)(2,1)S(1)} %fusion.37, s32[1280]{0:T(1024)S(1)} %add_select_fusion.2, pred[1280]{0:T(1024)(128)(4,1)S(1)} %get-tuple-element.11, pred[1280]{0:T(1024)(128)(4,1)S(1)} %get-tuple-element.12), kind=kOutput, calls=%fused_computation.26 | convolution fusion | flops 39333120 | bytes 51200 | tf_op jit(solution)/shard_map/dot_general | solution.py:70
  24.5 0.1 broadcast_in_dim.105
  24.6 25.9 %all_to_all.26 = bf16[16,3,3,1280]{3,1,2,0:T(4,128)(2,1)S(1)} all-to-all(bf16[16,3,3,1280]{3,1,2,0:T(4,128)(2,1)S(1)} %broadcast_in_dim.105), channel_id=1, replica_groups=mesh['row'=16,'col'=32] {'row'}, dimensions={0} | all-to-all | bytes 737280 | tf_op jit(solution)/shard_map/all_to_all | solution.py:13
  50.5 1.2 broadcast_in_dim.108
  51.7 12.1 %all-to-all-start.1 = ((bf16[32,3,3,1280]{3,1,2,0:T(4,128)(2,1)}), bf16[32,3,3,1280]{3,1,2,0:T(4,128)(2,1)S(1)}, u32[]{:S(2)}, u32[]{:S(2)}) async-start(bf16[32,3,3,1280]{3,1,2,0:T(4,128)(2,1)} %broadcast_in_dim.108), calls=%async_computation.1 | async-start | bytes 1966080 | tf_op jit(solution)/shard_map/all_to_all | solution.py:13
  63.9 13.3 %select_convert_fusion.11 = bf16[1280,512]{1,0:T(8,128)(2,1)} fusion(f32[1280]{0:T(1024)S(1)} %get-tuple-element.14, bf16[512]{0:T(512)(128)(2,1)S(1)} %select_multiply_fusion.1, s32[512]{0:T(512)S(1)} %iota_add_fusion, s32[1280]{0:T(1024)S(1)} %add_select_fusion.2, f32[1280]{0:T(1024)S(1)} %get-tuple-element.13, ...), kind=kLoop, calls=%fused_computation.17.clone.clone.2 | loop fusion | flops 8519680 | bytes 1331712 | tf_op jit(solution)/shard_map/dot_general | solution.py:99
  77.2 0.2 copy.15
  77.4 0.3 reshape.137
  77.7 0.1 broadcast_select_fusion.1
  77.8 1.3 copy.22
  79.2 1.8 %copy.20 = bf16[48,6,640]{0,1,2:T(8,128)(2,1)} copy(bf16[48,6,640]{2,0,1:T(8,128)(2,1)S(1)} %pad_maximum_fusion.4) | data formatting | bytes 737280 | tf_op jit(solution)/shard_map/concatenate | solution.py:90
  81.0 9.1 %all-to-all-done.1 = bf16[32,3,3,1280]{3,1,2,0:T(4,128)(2,1)S(1)} async-done(((bf16[32,3,3,1280]{3,1,2,0:T(4,128)(2,1)}), bf16[32,3,3,1280]{3,1,2,0:T(4,128)(2,1)S(1)}, u32[]{:S(2)}, u32[]{:S(2)}) %all-to-all-start.1) | async-done | bytes 737312 | tf_op jit(solution)/shard_map/all_to_all | solution.py:13
  90.1 1.3 copy.17
  91.4 2.3 %reshape.138 = bf16[96,3,1280]{2,0,1:T(8,128)(2,1)S(1)} reshape(bf16[32,3,3,1280]{3,1,0,2:T(4,128)(2,1)} %copy.17) | data formatting | bytes 1474560 | tf_op jit(solution)/shard_map/reshape | solution.py:19
  93.7 0.8 fusion.50
  94.6 0.8 copy.26
  95.4 2.4 %broadcast_select_fusion = bf16[96,3,640]{0,1,2:T(4,128)(2,1)S(1)} fusion(bf16[96,3,640]{0,1,2:T(4,128)(2,1)S(1)} %copy.26, pred[640]{0:T(1024)(128)(4,1)S(1)} %iota_compare_fusion.2), kind=kLoop, calls=%fused_computation.41 | loop fusion | flops 184320 | bytes 737920 | tf_op jit(solution)/shard_map/jit(_where)/select_n | solution.py:86
  97.8 1.7 %copy.27 = bf16[96,3,640]{0,1,2:T(4,128)(2,1)S(1)} copy(bf16[96,3,640]{2,0,1:T(8,128)(2,1)} %get-tuple-element.6) | data formatting | bytes 737280
  99.4 4.5 %convert_bitcast_fusion = bf16[96,48,640]{0,1,2:T(8,128)(2,1)} fusion(bf16[48,6,640]{0,1,2:T(8,128)(2,1)S(1)} %copy.22, bf16[96,3,640]{0,1,2:T(4,128)(2,1)S(1)} %copy.27, bf16[96,3,640]{0,1,2:T(4,128)(2,1)S(1)} %broadcast_select_fusion), kind=kOutput, calls=%fused_computation.4 | convolution fusion | flops 39813120 | bytes 7004160 | tf_op jit(solution)/shard_map/icf,jcf->ijf/dot_general | solution.py:75
  103.9 0.0 copy-start
  103.9 11.5 %copy.23 = bf16[96,48,640]{2,1,0:T(8,128)(2,1)} copy(bf16[96,48,640]{0,1,2:T(8,128)(2,1)} %convert_bitcast_fusion) | data formatting | bytes 11796480 | tf_op jit(solution)/shard_map/icf,jcf->ijf/transpose | solution.py:75
  115.4 0.0 copy-done
  115.4 4.5 %convert_bitcast_fusion.1 = bf16[96,48,640]{0,1,2:T(8,128)(2,1)} fusion(bf16[48,6,640]{0,1,2:T(8,128)(2,1)S(1)} %copy-done, bf16[96,3,640]{0,1,2:T(4,128)(2,1)S(1)} %copy.27, bf16[96,3,640]{0,1,2:T(4,128)(2,1)S(1)} %copy.26), kind=kOutput, calls=%fused_computation.5 | convolution fusion | flops 39813120 | bytes 7004160 | tf_op jit(solution)/shard_map/icf,jcf->ijf/dot_general | solution.py:75
  119.8 0.0 copy-start.1
  119.8 11.4 %copy.21 = bf16[96,48,640]{2,1,0:T(8,128)(2,1)} copy(bf16[96,48,640]{0,1,2:T(8,128)(2,1)} %convert_bitcast_fusion.1) | data formatting | bytes 11796480 | tf_op jit(solution)/shard_map/icf,jcf->ijf/transpose | solution.py:75
  131.2 0.0 copy-done.1
  131.2 9.6 %fusion.17 = f32[4608]{0:T(1024)S(1)} fusion(bf16[4608,640]{1,0:T(8,128)(2,1)} %bitcast.21, bf16[4608,640]{1,0:T(8,128)(2,1)} %bitcast.22, bf16[1280,512]{1,0:T(8,128)(2,1)S(1)} %copy-done.1), kind=kOutput, calls=%fused_computation.25 | convolution fusion | flops 6065745408 | bytes 13125632 | tf_op jit(solution)/shard_map/dot_general | solution.py:99
  140.9 0.1 all_to_all.20
  141.0 0.1 reshape.141
  141.1 14.0 %all_to_all.27 = f32[32,1,144]{2,1,0:T(1,128)S(1)} all-to-all(f32[32,1,144]{2,1,0:T(1,128)S(1)} %reshape.141), channel_id=1, replica_groups=mesh['row'=16,'col'=32] {'col'}, dimensions={0} | all-to-all | bytes 36864 | tf_op jit(solution)/shard_map/all_to_all | solution.py:119
  155.1 0.5 broadcast.247
  155.6 0.7 reduce
  156.3 0.1 reshape.142
  156.4 0.1 copy.24
  156.6 0.4 copy.25
  156.9 1.1 reshape.140
  (14 shorter events, 0.2 us)
Async XLA Ops:
  51.7 38.4 %all-to-all-start.1 = ((bf16[32,3,3,1280]{3,1,2,0:T(4,128)(2,1)}), bf16[32,3,3,1280]{3,1,2,0:T(4,128)(2,1)S(1)}, u32[]{:S(2)}, u32[]{:S(2)}) async-start(bf16[32,3,3,1280]{3,1,2,0:T(4,128)(2,1)} %broadcast_in_dim.108), calls=%async_computation.1 | async-start | bytes 1966080 | tf_op jit(solution)/shard_map/all_to_all | solution.py:13
  103.9 11.5 %copy-start = (bf16[48,6,640]{0,1,2:T(8,128)(2,1)S(1)}, bf16[48,6,640]{0,1,2:T(8,128)(2,1)}, u32[]{:S(2)}) copy-start(bf16[48,6,640]{0,1,2:T(8,128)(2,1)} %copy.20) | copy-start | bytes 1105924
  119.8 11.4 %copy-start.1 = (bf16[1280,512]{1,0:T(8,128)(2,1)S(1)}, bf16[1280,512]{1,0:T(8,128)(2,1)}, u32[]{:S(2)}) copy-start(bf16[1280,512]{1,0:T(8,128)(2,1)} %select_convert_fusion.11) | copy-start | bytes 3932164
where the time goes:
time: 159 us; the launch traced here: 158 us
  matrix products  41.2 us (26%)
  blocking collectives  39.9 us (25%)
  local copies, waits for them, and re-layouts  37.2 us (23%)
  other arithmetic  18.4 us (12%)
  starting transfers between devices  12.1 us (8%)
  waiting for transfers between devices  9.09 us (6%)
    all_to_all x1, blocking collectives, copy_for_each(): return lax.all_to_all(copies, axis, split_axis=0, concat_axis=0, tiled=True)  25.9 us
    transpose x2, local copies, waits for them, and re-layouts, pair_einsum(): jnp.einsum('icf,jcf->ijf', left_part.astype(jnp.float32), right_part.asty...  22.9 us
    dot_general x1, matrix products, spectra_of(): spectrum = jnp.dot(flattened, basis, preferred_element_type=jnp.float32)  22.6 us
    all_to_all x1, blocking collectives, body(): lax.all_to_all(pair_block, 'col', split_axis=0, concat_axis=1, tiled=True)  14 us
    dot_general x1, other arithmetic, similarity(): jnp.dot(cross_spec.reshape(left_rows * right_rows, 2 * half_len), inverse...  13.3 us
    all_to_all x1, starting transfers between devices, copy_for_each(): return lax.all_to_all(copies, axis, split_axis=0, concat_axis=0, tiled=True)  12.1 us
    dot_general x1, matrix products, similarity(): jnp.dot(cross_spec.reshape(left_rows * right_rows, 2 * half_len), inverse...  9.65 us
    all_to_all x1, waiting for transfers between devices, copy_for_each(): return lax.all_to_all(copies, axis, split_axis=0, concat_axis=0, tiled=True)  9.09 us
  transfers between devices with their start and end apart: 1, of which 1 were waited for; matrix products, arithmetic and copies ran while one was open for 11% of the time, Pallas kernels for 0%

commit v1 on v0

v1 whole, which is shorter than its diff:
```python
import functools
import math

import jax
import jax.numpy as jnp
import numpy as np
from jax import lax
from jax.experimental import pallas as pl
from jax.experimental.pallas import tpu as pltpu
from jax.sharding import PartitionSpec as P

LAGS = 512
LANES = 128


def forward_table(samples, transform_len):
    half_len = transform_len // 2
    sample_idx = np.arange(samples)[:, None]
    slot_idx = np.arange(transform_len)[None, :]
    freq_idx = np.where(slot_idx < half_len, slot_idx, slot_idx - half_len)
    phases = (sample_idx * freq_idx) % transform_len
    angles = phases * (2.0 * math.pi / transform_len)
    nyquist = np.where(sample_idx % 2 == 0, 1.0, -1.0)
    basis = np.where(
        slot_idx < half_len,
        np.cos(angles),
        np.where(slot_idx == half_len, nyquist, -np.sin(angles)),
    )
    return basis.astype(np.float32).astype(jnp.bfloat16)


def lag_tables(transform_len, half_lags):
    half_len = transform_len // 2
    freq_idx = np.arange(half_len)[:, None]
    lag_idx = np.concatenate([np.arange(0, half_lags, 2), np.arange(1, half_lags, 2)])[None, :]
    phases = (freq_idx * lag_idx) % transform_len
    angles = phases * (2.0 * math.pi / transform_len)
    weight = np.where(freq_idx == 0, 1.0, 2.0) / transform_len
    even = (weight * np.cos(angles)).astype(np.float32)
    odd = np.where(freq_idx == 0, 0.0, -weight * np.sin(angles)).astype(np.float32)
    return even.astype(jnp.bfloat16), odd.astype(jnp.bfloat16)


def normalize_kernel(copies, x_ref, one_ref, many_ref, rows_ref):
    per_device, comps, samples = x_ref.shape
    parts = samples // LANES
    for t in range(per_device):
        x = x_ref[t]
        scaling = lax.rsqrt(jnp.sum(x * x, axis=1, keepdims=True) / samples + 1e-06) / math.sqrt(samples)
        y = x * scaling
        for a in range(parts):
            rows_ref[pl.ds(t * comps * parts + a, comps, stride=parts), :] = y[:, a * LANES : (a + 1) * LANES]
    packed = rows_ref[...].astype(jnp.bfloat16)
    one_ref[...] = packed
    for q in range(copies):
        many_ref[q] = packed


def normalize(templates, copies):
    per_device, comps, samples = templates.shape
    rows = per_device * comps * samples // LANES
    return pl.pallas_call(
        functools.partial(normalize_kernel, copies),
        out_shape=(
            jax.ShapeDtypeStruct((rows, LANES), jnp.bfloat16),
            jax.ShapeDtypeStruct((copies, rows, LANES), jnp.bfloat16),
        ),
        scratch_shapes=[pltpu.VMEM((rows, LANES), jnp.float32)],
        compiler_params=pltpu.CompilerParams(vmem_limit_bytes=8 << 20),
        name="normalize",
    )(templates)


def similarity_kernel(
    comps, samples, chunk, step, *refs
):
    (left_ref, right_ref, basis_ref, even_ref, odd_ref, out_ref,
     rows_ref, lw_ref, rw_ref, lr_ref, li_ref, ls_ref, rr_ref, ri_ref, rd_ref,
     ce0, co0, ce1, co1, me_ref, mo_ref) = refs
    parts = samples // LANES
    left = left_ref.shape[0] // (comps * parts)
    right = right_ref.shape[0] // (comps * parts)
    half_len = even_ref.shape[0]
    tiles = half_len // LANES

    def waves(src_ref, wave_ref, count):
        total = count * comps * parts
        rows_ref[0:total, :] = src_ref[...].astype(jnp.float32)
        for c in range(comps):
            for a in range(parts):
                wave_ref[c * count : (c + 1) * count, a * LANES : (a + 1) * LANES] = rows_ref[
                    pl.ds(c * parts + a, count, stride=comps * parts), :
                ].astype(jnp.bfloat16)

    waves(left_ref, lw_ref, left)
    waves(right_ref, rw_ref, right)

    def spectrum(wave_ref):
        return jnp.dot(wave_ref[...], basis_ref[...], preferred_element_type=jnp.float32)

    first = lax.broadcasted_iota(jnp.int32, (1, half_len), 1) == 0

    def split(spec):
        rounded = spec.astype(jnp.bfloat16).astype(jnp.float32)
        slots = rounded[:, half_len:]
        top = jnp.where(first[:, :LANES], slots[:, :LANES], 0.0)
        return rounded[:, :half_len], jnp.where(first, 0.0, slots), top

    real, imag, top_left = split(spectrum(lw_ref))
    for f in range(tiles):
        fs = slice(f * LANES, (f + 1) * LANES)
        lr_ref[f] = real[:, fs]
        li_ref[f] = imag[:, fs]
        ls_ref[f] = real[:, fs] + imag[:, fs]
    real, imag, top_right = split(spectrum(rw_ref))
    rr_ref[...] = real
    ri_ref[...] = imag
    rd_ref[...] = imag - real

    nt = (((1,), (1,)), ((), ()))
    shift = LAGS // 2
    highest = jnp.zeros((right, left), jnp.float32)
    earliest = jnp.zeros((right, left), jnp.float32)
    for c in range(comps):
        lsl, rsl = slice(c * left, (c + 1) * left), slice(c * right, (c + 1) * right)
        highest += lax.dot_general(
            top_right[rsl].astype(jnp.bfloat16), top_left[lsl].astype(jnp.bfloat16), nt,
            preferred_element_type=jnp.float32,
        )
        earliest += lax.dot_general(
            rw_ref[rsl, : samples - shift], lw_ref[lsl, shift:], nt,
            preferred_element_type=jnp.float32,
        )

    def cross(index, even_out, odd_out):
        for f in range(tiles):
            fs = slice(f * LANES, (f + 1) * LANES)
            for u in range(chunk):
                i = index * chunk + u
                lr = [lr_ref[f, pl.ds(c * left + i, 1), :] for c in range(comps)]
                li = [li_ref[f, pl.ds(c * left + i, 1), :] for c in range(comps)]
                ls = [ls_ref[f, pl.ds(c * left + i, 1), :] for c in range(comps)]
                for j in range(0, right, step):
                    rr = rr_ref[j : j + step, fs] * lr[0]
                    ii = ri_ref[j : j + step, fs] * li[0]
                    mm = rd_ref[j : j + step, fs] * ls[0]
                    for c in range(1, comps):
                        rows = slice(c * right + j, c * right + j + step)
                        rr += rr_ref[rows, fs] * lr[c]
                        ii += ri_ref[rows, fs] * li[c]
                        mm += rd_ref[rows, fs] * ls[c]
                    rows = slice(u * right + j, u * right + j + step)
                    even_out[rows, fs] = (rr + ii).astype(jnp.bfloat16)
                    odd_out[rows, fs] = (mm + (rr - ii)).astype(jnp.bfloat16)

    column = lax.broadcasted_iota(jnp.int32, (1, left), 1)

    def lags(index, even_in, odd_in):
        even = jnp.dot(even_in[...], even_ref[...], preferred_element_type=jnp.float32)
        odd = jnp.dot(odd_in[...], odd_ref[...], preferred_element_type=jnp.float32)
        best = even + jnp.abs(odd)
        for u in range(chunk):
            here = column == index * chunk + u
            rows = best[u * right : (u + 1) * right]
            me_ref[...] = jnp.where(here, jnp.max(rows[:, :LANES], axis=1, keepdims=True), me_ref[...])
            mo_ref[...] = jnp.where(here, jnp.max(rows[:, LANES:], axis=1, keepdims=True), mo_ref[...])

    me_ref[...] = jnp.zeros_like(me_ref)
    mo_ref[...] = jnp.zeros_like(mo_ref)
    count = left // chunk
    cross(0, ce0, co0)

    def both(n, carry):
        cross(2 * n + 1, ce1, co1)
        lags(2 * n, ce0, co0)
        cross(jnp.minimum(2 * n + 2, count - 1), ce0, co0)
        lags(2 * n + 1, ce1, co1)
        return carry

    lax.fori_loop(0, count // 2, both, 0)

    alternating = highest.astype(jnp.bfloat16).astype(jnp.float32) / (2 * half_len)
    best = jnp.maximum(me_ref[...] + alternating, mo_ref[...] - alternating)
    best = jnp.maximum(best, earliest)
    wide = jnp.concatenate([best, jnp.zeros((right, LANES - left), jnp.float32)], axis=1)
    tall = jnp.concatenate([wide, jnp.zeros((LANES - right, LANES), jnp.float32)], axis=0)
    turned = tall.T
    owners, per_owner = out_ref.shape[0], left // out_ref.shape[0]
    for r in range(owners):
        out_ref[r, 0:per_owner, :] = turned[r * per_owner : (r + 1) * per_owner, :]


def similarity(left_waves, right_waves, comps, samples, owners):
    transform_len = samples + LAGS // 2
    half_len = transform_len // 2
    parts = samples // LANES
    left = left_waves.shape[0] // (comps * parts)
    right = right_waves.shape[0] // (comps * parts)
    basis = jnp.asarray(forward_table(samples, transform_len))
    even, odd = (jnp.asarray(t) for t in lag_tables(transform_len, LAGS // 2))
    chunk, step = 2, 32
    f32, bf16 = jnp.float32, jnp.bfloat16
    return pl.pallas_call(
        functools.partial(similarity_kernel, comps, samples, chunk, step),
        out_shape=jax.ShapeDtypeStruct((owners, 8, LANES), f32),
        scratch_shapes=[
            pltpu.VMEM((right * comps * parts, LANES), f32),
            pltpu.VMEM((left * comps, samples), bf16),
            pltpu.VMEM((right * comps, samples), bf16),
            *[pltpu.VMEM((half_len // LANES, left * comps, LANES), f32)] * 3,
            *[pltpu.VMEM((right * comps, half_len), f32)] * 3,
            *[pltpu.VMEM((chunk * right, half_len), bf16)] * 4,
            *[pltpu.VMEM((right, left), f32)] * 2,
        ],
        compiler_params=pltpu.CompilerParams(vmem_limit_bytes=28 << 20),
        cost_estimate=pl.CostEstimate(flops=8_000_000_000, bytes_accessed=4_000_000, transcendentals=0),
        name="similarity",
    )(left_waves, right_waves, basis, even, odd)


def assemble_kernel(width, in_ref, out_ref):
    for r in range(in_ref.shape[0]):
        out_ref[:, r * width : (r + 1) * width] = in_ref[r, 0 : out_ref.shape[0], 0:width]


def body(templates):
    per_device, comps, samples = templates.shape
    row_count = lax.axis_size("row")
    col_count = lax.axis_size("col")
    one, many = normalize(templates, col_count)
    partners = lax.all_to_all(many, "col", split_axis=0, concat_axis=0, tiled=True)
    owned = lax.all_gather(one, "row", tiled=True)
    partners = partners.reshape(col_count * one.shape[0], LANES)
    block = similarity(owned, partners, comps, samples, row_count)
    mine = lax.all_to_all(block, "row", split_axis=0, concat_axis=0, tiled=True)
    width = col_count * per_device
    return pl.pallas_call(
        functools.partial(assemble_kernel, width),
        out_shape=jax.ShapeDtypeStruct((per_device, row_count * width), jnp.float32),
        name="assemble",
    )(mine)


def solution(mesh):
    placed = (P(("row", "col"), None, None),)
    return jax.shard_map(
        body, mesh=mesh, in_specs=placed, out_specs=P(("row", "col"), None), check_vma=False
    )
```

time: 159 us -> 70.4 us (0.44)
  matrix products: 41.2 us -> 0 us
  local copies, waits for them, and re-layouts: 37.2 us -> 4.48 us
  other arithmetic: 18.4 us -> 0 us
  Pallas kernels: 0 us -> 17 us
  waiting for transfers between devices: 9.09 us -> 0.01 us
  blocking collectives: 39.9 us -> 34.7 us
  starting transfers between devices: 12.1 us -> 13.7 us
    dot_general x4 -> x0, matrix products: 41.2 us -> none  [the longest x1 22.6 us: spectra_of(): spectrum = jnp.dot(flattened, basis, preferred_element_type=jnp.float32)]
    all_to_all x2 -> x1, blocking collectives: 39.9 us -> 15.5 us  [body(): mine = lax.all_to_all(block, 'row', split_axis=0, concat_axis=0, tiled=True)]
    transpose x3 -> x0, local copies, waits for them, and re-layouts: 23.2 us -> none  [the longest x2 22.9 us: pair_einsum(): jnp.einsum('icf,jcf->ijf', left_part.astype(jnp.float32), right_part.asty...]
    all_gather x0 -> x1, blocking collectives: none -> 19.2 us  [body(): owned = lax.all_gather(one, 'row', tiled=True)]
    pallas_call x0 -> x3, Pallas kernels: none -> 17 us  [the longest x1 14.5 us: similarity(): pl.pallas_call(functools.partial(similarity_kernel, comps, samples, chunk...]
    dot_general x1 -> x0, other arithmetic: 13.3 us -> none  [similarity(): jnp.dot(cross_spec.reshape(left_rows * right_rows, 2 * half_len), inverse...]
    all_to_all x1, waiting for transfers between devices: 9.09 us -> 0.01 us  [body(): lax.all_to_all(many, 'col', split_axis=0, concat_axis=0, tiled=True)]
    reshape x7 -> x0, local copies, waits for them, and re-layouts: 3.81 us -> none  [the longest x2 2.63 us: in_order(): return jnp.moveaxis(tiles, 0, dim).reshape(shape)]
  transfers between devices with their start and end apart: 1 -> 1, of which waited for: 1 -> 0; matrix products, arithmetic and copies ran while one was open for 11% -> 0% of each run, Pallas kernels for 0% -> 0%
where the time goes in v1:
time: 70.4 us; the launch traced here: 70 us
  blocking collectives  34.7 us (49%)
  Pallas kernels  17 us (24%)
  starting transfers between devices  13.7 us (19%)
  local copies, waits for them, and re-layouts  4.48 us (6%)
    all_gather x1, blocking collectives, body(): owned = lax.all_gather(one, 'row', tiled=True)  19.2 us
    all_to_all x1, blocking collectives, body(): mine = lax.all_to_all(block, 'row', split_axis=0, concat_axis=0, tiled=True)  15.5 us
    pallas_call x1, Pallas kernels, similarity(): pl.pallas_call(functools.partial(similarity_kernel, comps, samples, chunk...  14.5 us
    all_to_all x1, starting transfers between devices, body(): lax.all_to_all(many, 'col', split_axis=0, concat_axis=0, tiled=True)  13.7 us
    unnamed x8, local copies, waits for them, and re-layouts  4.48 us
    pallas_call x1, Pallas kernels, body(): pl.pallas_call(functools.partial(assemble_kernel, width), out_shape=jax.S...  1.53 us
  transfers between devices with their start and end apart: 1, of which 0 were waited for; matrix products, arithmetic and copies ran while one was open for 0% of the time, Pallas kernels for 0%

profile of v1, /device:TPU:1, one launch (start us, length us, event | category | flops | bytes accessed | tf_op | source)
XLA Modules:
  0.0 70.0 jit_solution(16784640608757606977)
XLA Ops:
  0.0 0.0 copy-start
  0.0 0.8 %copy-done = f32[3,3,1024]{2,1,0:T(4,128)S(1)} copy-done((f32[3,3,1024]{2,1,0:T(4,128)S(1)}, f32[3,3,1024]{2,1,0:T(4,128)}, u32[]{:S(2)}) %copy-start) | copy-done | bytes 36888
  0.8 1.0 %normalize.1 = (bf16[72,128]{1,0:T(8,128)(2,1)S(1)}, bf16[32,72,128]{2,1,0:T(8,128)(2,1)}) custom-call(f32[3,3,1024]{2,1,0:T(4,128)S(1)} %copy-done), custom_call_target="tpu_custom_call" | custom-call | tf_op jit(solution)/shard_map/normalize/pallas_call | solution.py:62
  1.8 13.7 %all-to-all-start = ((bf16[32,72,128]{2,1,0:T(8,128)(2,1)}), bf16[32,72,128]{2,1,0:T(8,128)(2,1)S(1)}, u32[]{:S(2)}, u32[]{:S(2)}) async-start(bf16[32,72,128]{2,1,0:T(8,128)(2,1)} %get-tuple-element.8), calls=%async_computation | async-start | bytes 1179648 | tf_op jit(solution)/shard_map/all_to_all | solution.py:231
  15.5 19.2 %all_gather.3.refs_0_ = bf16[1152,128]{1,0:T(8,128)(2,1)S(1)} all-gather(bf16[72,128]{1,0:T(8,128)(2,1)S(1)} %get-tuple-element.7), channel_id=1, replica_groups=mesh['row'=16,'col'=32] {'row'}, dimensions={0}, use_global_device_ids=true | all-gather | bytes 313344 | tf_op jit(solution)/shard_map/all_gather | solution.py:232
  34.7 0.0 all-to-all-done
  34.7 0.0 copy-start.1
  34.7 1.7 %copy-done.1 = bf16[1024,1280]{1,0:T(8,128)(2,1)S(1)} copy-done((bf16[1024,1280]{1,0:T(8,128)(2,1)S(1)}, bf16[1024,1280]{1,0:T(8,128)(2,1)}, u32[]{:S(2)}) %copy-start.1) | copy-done | bytes 2621464
  36.4 0.0 copy-start.2
  36.4 1.0 %copy-done.2 = bf16[640,256]{1,0:T(8,128)(2,1)S(1)} copy-done((bf16[640,256]{1,0:T(8,128)(2,1)S(1)}, bf16[640,256]{1,0:T(8,128)(2,1)}, u32[]{:S(2)}) %copy-start.2) | copy-done | bytes 327704
  37.4 0.0 copy-start.3
  37.4 1.0 %copy-done.3 = bf16[640,256]{1,0:T(8,128)(2,1)S(1)} copy-done((bf16[640,256]{1,0:T(8,128)(2,1)S(1)}, bf16[640,256]{1,0:T(8,128)(2,1)}, u32[]{:S(2)}) %copy-start.3) | copy-done | bytes 327704
  38.4 14.5 %similarity.1 = f32[16,8,128]{2,1,0:T(8,128)S(1)} custom-call(bf16[1152,128]{1,0:T(8,128)(2,1)S(1)} %all_gather.3.refs_0_, bf16[2304,128]{1,0:T(8,128)(2,1)S(1)} %bitcast.1, bf16[1024,1280]{1,0:T(8,128)(2,1)S(1)} %copy-done.1, bf16[640,256]{1,0:T(8,128)(2,1)S(1)} %copy-done.3, bf16[640,256]{1,0:T(8,128)(2,1)S(1)} %copy-done.2), custom_call_target="tpu_custom_call" | custom-call | flops 8000000000 | bytes 4000000 | tf_op jit(solution)/shard_map/similarity/pallas_call | solution.py:203
  52.9 15.5 %all_to_all.10.in_ref = f32[16,8,128]{2,1,0:T(8,128)} all-to-all(f32[16,8,128]{2,1,0:T(8,128)S(1)} %similarity.1), channel_id=1, replica_groups=mesh['row'=16,'col'=32] {'row'}, dimensions={0} | all-to-all | bytes 131072 | tf_op jit(solution)/shard_map/all_to_all | solution.py:235
  68.4 1.5 %assemble.1 = f32[3,1536]{1,0:T(4,128)} custom-call(f32[16,8,128]{2,1,0:T(8,128)} %all_to_all.10.in_ref), custom_call_target="tpu_custom_call" | custom-call | tf_op jit(solution)/shard_map/assemble/pallas_call | solution.py:237
Async XLA Ops:
  0.0 0.8 %copy-start = (f32[3,3,1024]{2,1,0:T(4,128)S(1)}, f32[3,3,1024]{2,1,0:T(4,128)}, u32[]{:S(2)}) copy-start(f32[3,3,1024]{2,1,0:T(4,128)} %x_ref.1) | copy-start | bytes 110596
  1.8 32.9 %all-to-all-start = ((bf16[32,72,128]{2,1,0:T(8,128)(2,1)}), bf16[32,72,128]{2,1,0:T(8,128)(2,1)S(1)}, u32[]{:S(2)}, u32[]{:S(2)}) async-start(bf16[32,72,128]{2,1,0:T(8,128)(2,1)} %get-tuple-element.8), calls=%async_computation | async-start | bytes 1179648 | tf_op jit(solution)/shard_map/all_to_all | solution.py:231
  34.7 1.7 %copy-start.1 = (bf16[1024,1280]{1,0:T(8,128)(2,1)S(1)}, bf16[1024,1280]{1,0:T(8,128)(2,1)}, u32[]{:S(2)}) copy-start(bf16[1024,1280]{1,0:T(8,128)(2,1)} %constant.6.clone.refs_2_) | copy-start | bytes 7864324
  36.4 1.0 %copy-start.2 = (bf16[640,256]{1,0:T(8,128)(2,1)S(1)}, bf16[640,256]{1,0:T(8,128)(2,1)}, u32[]{:S(2)}) copy-start(bf16[640,256]{1,0:T(8,128)(2,1)} %constant.8.clone.refs_4_) | copy-start | bytes 983044
  37.4 1.0 %copy-start.3 = (bf16[640,256]{1,0:T(8,128)(2,1)S(1)}, bf16[640,256]{1,0:T(8,128)(2,1)}, u32[]{:S(2)}) copy-start(bf16[640,256]{1,0:T(8,128)(2,1)} %constant.7.clone.refs_3_) | copy-start | bytes 983044

commit v2 on v1

v2 whole, which is shorter than its diff:
```python
import functools
import math

import jax
import jax.numpy as jnp
import numpy as np
from jax import lax
from jax.experimental import pallas as pl
from jax.experimental.pallas import tpu as pltpu
from jax.sharding import PartitionSpec as P

LAGS = 512
LANES = 128


def frequency_order(half_len):
    quarter, whole = half_len // 2, half_len // 2 // LANES * LANES
    even, odd = 2 * np.arange(quarter), 2 * np.arange(quarter) + 1
    return np.concatenate([even[:whole], even[whole:], odd[whole:], odd[:whole]])


def transform_tables(transform_len, half_lags):
    half_len = transform_len // 2
    step = 2.0 * math.pi / transform_len
    order = frequency_order(half_len)
    whole = half_len // 2 // LANES * LANES
    rest = half_len // 2 - whole
    sample = np.arange(half_len)[:, None]
    angles = (sample * order[None, :]) % transform_len * step
    real = np.cos(angles)
    imag = np.where(order[None, :] == 0, np.where(sample % 2 == 0, 1.0, -1.0), -np.sin(angles))
    evens, evens_rest = slice(0, whole), slice(whole, whole + rest)
    odds_rest, odds = slice(whole + rest, half_len - whole), slice(half_len - whole, half_len)
    forward = [real[:, evens], imag[:, evens], real[:, evens_rest], imag[:, evens_rest]]
    forward += [real[:, odds], imag[:, odds], real[:, odds_rest], imag[:, odds_rest]]
    lag = np.concatenate([np.arange(0, half_lags, 2), np.arange(1, half_lags, 2)])[None, :]
    angles = (order[:, None] * lag) % transform_len * step
    weight = np.where(order[:, None] == 0, 1.0, 2.0) / transform_len
    cosine = weight * np.cos(angles)
    sine = np.where(order[:, None] == 0, 0.0, -weight * np.sin(angles))
    return np.concatenate([*forward, cosine, sine], axis=1).astype(np.float32).astype(jnp.bfloat16)


def normalize_kernel(copies, x_ref, one_ref, many_ref, rows_ref):
    per_device, comps, samples = x_ref.shape
    parts = samples // LANES
    for t in range(per_device):
        x = x_ref[t]
        scaling = lax.rsqrt(jnp.sum(x * x, axis=1, keepdims=True) / samples + 1e-06) / math.sqrt(samples)
        y = x * scaling
        for a in range(parts):
            rows_ref[pl.ds(t * comps * parts + a, comps, stride=parts), :] = y[:, a * LANES : (a + 1) * LANES]
    packed = rows_ref[...].astype(jnp.bfloat16)
    one_ref[...] = packed
    for q in range(copies):
        many_ref[q] = packed


def normalize(templates, copies):
    per_device, comps, samples = templates.shape
    rows = per_device * comps * samples // LANES
    return pl.pallas_call(
        functools.partial(normalize_kernel, copies),
        out_shape=(
            jax.ShapeDtypeStruct((rows, LANES), jnp.bfloat16),
            jax.ShapeDtypeStruct((copies, rows, LANES), jnp.bfloat16),
        ),
        scratch_shapes=[pltpu.VMEM((rows, LANES), jnp.float32)],
        compiler_params=pltpu.CompilerParams(vmem_limit_bytes=8 << 20),
        name="normalize",
    )(templates)


def similarity_kernel(comps, samples, chunk, step, *refs):
    (left_ref, right_ref, tables_hbm, out_ref,
     basis_ref, even_ref, odd_ref, rows_ref, wave_ref,
     l1_ref, l2_ref, l3_ref, r1_ref, r2_ref, r3_ref,
     ce0, co0, ce1, co1, me_ref, mo_ref, sems) = refs
    parts = samples // LANES
    left = left_ref.shape[0] // (comps * parts)
    right = right_ref.shape[0] // (comps * parts)
    half_len, lag_count = even_ref.shape
    tiles = half_len // LANES

    width = 2 * half_len
    sources = [slice(0, width), slice(width, width + lag_count), slice(width + lag_count, width + 2 * lag_count)]
    copies = [
        pltpu.make_async_copy(tables_hbm.at[:, source], target, sems.at[k])
        for k, (source, target) in enumerate(zip(sources, (basis_ref, even_ref, odd_ref)))
    ]
    for copy in copies:
        copy.start()

    def waves(src_ref, base, count):
        total = count * comps * parts
        rows_ref[0:total, :] = src_ref[...].astype(jnp.float32)
        for c in range(comps):
            for a in range(parts):
                wave_ref[base + c * count : base + (c + 1) * count, a * LANES : (a + 1) * LANES] = rows_ref[
                    pl.ds(c * parts + a, count, stride=comps * parts), :
                ].astype(jnp.bfloat16)

    split = comps * left
    waves(left_ref, 0, left)
    waves(right_ref, split, right)

    nt = (((1,), (1,)), ((), ()))
    shift = LAGS // 2
    earliest = jnp.zeros((right, left), jnp.float32)
    for c in range(comps):
        earliest += lax.dot_general(
            wave_ref[split + c * right : split + (c + 1) * right, : samples - shift],
            wave_ref[c * left : (c + 1) * left, shift:],
            nt, preferred_element_type=jnp.float32,
        )

    copies[0].wait()
    tail = samples - half_len

    def product(cols):
        low = jnp.dot(wave_ref[:, :half_len], basis_ref[:, cols], preferred_element_type=jnp.float32)
        high = jnp.dot(wave_ref[:, half_len:], basis_ref[:tail, cols], preferred_element_type=jnp.float32)
        return low, high

    def rounded(values):
        return values.astype(jnp.bfloat16).astype(jnp.float32)

    low, high = product(slice(0, half_len))
    evens = rounded(low + high)
    low, high = product(slice(half_len, width))
    odds = rounded(low - high)
    whole = half_len // 2 // LANES
    lane = lax.broadcasted_iota(jnp.int32, (1, LANES), 1)

    def tile(values, k):
        return values[:, k * LANES : (k + 1) * LANES]

    def parts_of(f):
        if f < whole:
            return tile(evens, f), tile(evens, whole + f)
        if f > whole:
            return tile(odds, f - whole - 1), tile(odds, f - 1)
        a, b = tile(evens, 2 * whole), tile(odds, 2 * whole)
        half = LANES // 2
        return (
            jnp.where(lane < half, a, pltpu.roll(b, half, 1)),
            jnp.where(lane < half, pltpu.roll(a, half, 1), b),
        )

    top = None
    for f in range(tiles):
        fs = slice(f * LANES, (f + 1) * LANES)
        real, imag = parts_of(f)
        if f == 0:
            top = jnp.where(lane == 0, imag, 0.0).astype(jnp.bfloat16)
            imag = jnp.where(lane == 0, 0.0, imag)
        l1_ref[f] = real[:split]
        l2_ref[f] = real[:split] - imag[:split]
        l3_ref[f] = real[:split] + imag[:split]
        r1_ref[:, fs] = real[split:] + imag[split:]
        r2_ref[:, fs] = imag[split:]
        r3_ref[:, fs] = real[split:]
    highest = jnp.zeros((right, left), jnp.float32)
    for c in range(comps):
        highest += lax.dot_general(
            top[split + c * right : split + (c + 1) * right], top[c * left : (c + 1) * left],
            nt, preferred_element_type=jnp.float32,
        )

    def cross(index, even_out, odd_out):
        for f in range(tiles):
            fs = slice(f * LANES, (f + 1) * LANES)
            for u in range(chunk):
                i = index * chunk + u
                l1 = [l1_ref[f, pl.ds(c * left + i, 1), :] for c in range(comps)]
                l2 = [l2_ref[f, pl.ds(c * left + i, 1), :] for c in range(comps)]
                l3 = [l3_ref[f, pl.ds(c * left + i, 1), :] for c in range(comps)]
                for j in range(0, right, step):
                    k1 = r1_ref[j : j + step, fs] * l1[0]
                    k2 = r2_ref[j : j + step, fs] * l2[0]
                    k3 = r3_ref[j : j + step, fs] * l3[0]
                    for c in range(1, comps):
                        rows = slice(c * right + j, c * right + j + step)
                        k1 += r1_ref[rows, fs] * l1[c]
                        k2 += r2_ref[rows, fs] * l2[c]
                        k3 += r3_ref[rows, fs] * l3[c]
                    rows = slice(u * right + j, u * right + j + step)
                    even_out[rows, fs] = (k1 - k2).astype(jnp.bfloat16)
                    odd_out[rows, fs] = (k1 - k3).astype(jnp.bfloat16)

    column = lax.broadcasted_iota(jnp.int32, (1, left), 1)

    def lags(index, even_in, odd_in):
        even = jnp.dot(even_in[...], even_ref[...], preferred_element_type=jnp.float32)
        odd = jnp.dot(odd_in[...], odd_ref[...], preferred_element_type=jnp.float32)
        best = even + jnp.abs(odd)
        for u in range(chunk):
            here = column == index * chunk + u
            rows = best[u * right : (u + 1) * right]
            me_ref[...] = jnp.where(here, jnp.max(rows[:, :LANES], axis=1, keepdims=True), me_ref[...])
            mo_ref[...] = jnp.where(here, jnp.max(rows[:, LANES:], axis=1, keepdims=True), mo_ref[...])

    me_ref[...] = jnp.zeros_like(me_ref)
    mo_ref[...] = jnp.zeros_like(mo_ref)
    count = left // chunk
    cross(0, ce0, co0)
    copies[1].wait()
    copies[2].wait()

    def both(n, carry):
        cross(2 * n + 1, ce1, co1)
        lags(2 * n, ce0, co0)
        cross(jnp.minimum(2 * n + 2, count - 1), ce0, co0)
        lags(2 * n + 1, ce1, co1)
        return carry

    lax.fori_loop(0, count // 2, both, 0)

    alternating = highest.astype(jnp.bfloat16).astype(jnp.float32) / (2 * half_len)
    best = jnp.maximum(me_ref[...] + alternating, mo_ref[...] - alternating)
    best = jnp.maximum(best, earliest)
    wide = jnp.concatenate([best, jnp.zeros((right, LANES - left), jnp.float32)], axis=1)
    tall = jnp.concatenate([wide, jnp.zeros((LANES - right, LANES), jnp.float32)], axis=0)
    turned = tall.T
    owners, per_owner = out_ref.shape[0], left // out_ref.shape[0]
    for r in range(owners):
        out_ref[r, 0:per_owner, :] = turned[r * per_owner : (r + 1) * per_owner, :]


def similarity(left_waves, right_waves, comps, samples, owners):
    transform_len = samples + LAGS // 2
    half_len = transform_len // 2
    parts = samples // LANES
    left = left_waves.shape[0] // (comps * parts)
    right = right_waves.shape[0] // (comps * parts)
    tables = jnp.asarray(transform_tables(transform_len, LAGS // 2))
    chunk, step = 4, 32
    f32, bf16 = jnp.float32, jnp.bfloat16
    return pl.pallas_call(
        functools.partial(similarity_kernel, comps, samples, chunk, step),
        out_shape=jax.ShapeDtypeStruct((owners, 8, LANES), f32),
        in_specs=[pl.BlockSpec(memory_space=pltpu.VMEM)] * 2 + [pl.BlockSpec(memory_space=pltpu.HBM)],
        scratch_shapes=[
            pltpu.VMEM((half_len, transform_len), bf16),
            *[pltpu.VMEM((half_len, LAGS // 2), bf16)] * 2,
            pltpu.VMEM((right * comps * parts, LANES), f32),
            pltpu.VMEM(((left + right) * comps, samples), bf16),
            *[pltpu.VMEM((half_len // LANES, left * comps, LANES), f32)] * 3,
            *[pltpu.VMEM((right * comps, half_len), f32)] * 3,
            *[pltpu.VMEM((chunk * right, half_len), bf16)] * 4,
            *[pltpu.VMEM((right, left), f32)] * 2,
            pltpu.SemaphoreType.DMA((3,)),
        ],
        compiler_params=pltpu.CompilerParams(vmem_limit_bytes=54_500_000),
        cost_estimate=pl.CostEstimate(flops=8_000_000_000, bytes_accessed=4_000_000, transcendentals=0),
        name="similarity",
    )(left_waves, right_waves, tables)


def assemble_kernel(width, in_ref, out_ref):
    for r in range(in_ref.shape[0]):
        out_ref[:, r * width : (r + 1) * width] = in_ref[r, 0 : out_ref.shape[0], 0:width]


def body(templates):
    per_device, comps, samples = templates.shape
    row_count = lax.axis_size("row")
    col_count = lax.axis_size("col")
    one, many = normalize(templates, col_count)
    partners = lax.all_to_all(many, "col", split_axis=0, concat_axis=0, tiled=True)
    owned = lax.all_gather(one, "row", tiled=True)
    partners = partners.reshape(col_count * one.shape[0], LANES)
    block = similarity(owned, partners, comps, samples, row_count)
    mine = lax.all_to_all(block, "row", split_axis=0, concat_axis=0, tiled=True)
    width = col_count * per_device
    return pl.pallas_call(
        functools.partial(assemble_kernel, width),
        out_shape=jax.ShapeDtypeStruct((per_device, row_count * width), jnp.float32),
        compiler_params=pltpu.CompilerParams(vmem_limit_bytes=4 << 20),
        name="assemble",
    )(mine)


def solution(mesh):
    placed = (P(("row", "col"), None, None),)
    return jax.shard_map(
        body, mesh=mesh, in_specs=placed, out_specs=P(("row", "col"), None), check_vma=False
    )
```

time: 70.4 us -> 66.5 us (0.945)
  local copies, waits for them, and re-layouts: 4.48 us -> 0.8 us
    unnamed x8 -> x2, local copies, waits for them, and re-layouts: 4.48 us -> 0.8 us
    pallas_call x1, Pallas kernels: 14.5 us -> 15.4 us  [similarity(): pl.pallas_call(functools.partial(similarity_kernel, comps, samples, chunk...]
    pallas_call x1, Pallas kernels: 1.53 us -> 0.69 us  [body(): pl.pallas_call(functools.partial(assemble_kernel, width), out_shape=jax.S...]
where the time goes in v2:
time: 66.5 us; the launch traced here: 66.2 us
  blocking collectives  34.6 us (52%)
  Pallas kernels  17 us (26%)
  starting transfers between devices  13.7 us (21%)
  local copies, waits for them, and re-layouts  0.8 us (1%)
    all_gather x1, blocking collectives, body(): owned = lax.all_gather(one, 'row', tiled=True)  19.2 us
    all_to_all x1, blocking collectives, body(): mine = lax.all_to_all(block, 'row', split_axis=0, concat_axis=0, tiled=True)  15.4 us
    pallas_call x1, Pallas kernels, similarity(): pl.pallas_call(functools.partial(similarity_kernel, comps, samples, chunk...  15.4 us
    all_to_all x1, starting transfers between devices, body(): lax.all_to_all(many, 'col', split_axis=0, concat_axis=0, tiled=True)  13.7 us
  transfers between devices with their start and end apart: 1, of which 0 were waited for; matrix products, arithmetic and copies ran while one was open for 0% of the time, Pallas kernels for 0%

profile of v2, /device:TPU:1, one launch (start us, length us, event | category | flops | bytes accessed | tf_op | source)
XLA Modules:
  0.0 66.2 jit_solution(12082546004951145874)
XLA Ops:
  0.0 0.0 copy-start
  0.0 0.8 %copy-done = f32[3,3,1024]{2,1,0:T(4,128)S(1)} copy-done((f32[3,3,1024]{2,1,0:T(4,128)S(1)}, f32[3,3,1024]{2,1,0:T(4,128)}, u32[]{:S(2)}) %copy-start) | copy-done | bytes 36888
  0.8 1.0 %normalize.1 = (bf16[72,128]{1,0:T(8,128)(2,1)S(1)}, bf16[32,72,128]{2,1,0:T(8,128)(2,1)}) custom-call(f32[3,3,1024]{2,1,0:T(4,128)S(1)} %copy-done), custom_call_target="tpu_custom_call" | custom-call | tf_op jit(solution)/shard_map/normalize/pallas_call | solution.py:62
  1.8 13.7 %all-to-all-start = ((bf16[32,72,128]{2,1,0:T(8,128)(2,1)}), bf16[32,72,128]{2,1,0:T(8,128)(2,1)S(1)}, u32[]{:S(2)}, u32[]{:S(2)}) async-start(bf16[32,72,128]{2,1,0:T(8,128)(2,1)} %get-tuple-element.8), calls=%async_computation | async-start | bytes 1179648 | tf_op jit(solution)/shard_map/all_to_all | solution.py:270
  15.5 19.2 %all_gather.3.refs_0_ = bf16[1152,128]{1,0:T(8,128)(2,1)S(1)} all-gather(bf16[72,128]{1,0:T(8,128)(2,1)S(1)} %get-tuple-element.7), channel_id=1, replica_groups=mesh['row'=16,'col'=32] {'row'}, dimensions={0}, use_global_device_ids=true | all-gather | bytes 313344 | tf_op jit(solution)/shard_map/all_gather | solution.py:271
  34.7 0.0 all-to-all-done
  34.7 15.4 %similarity.1 = f32[16,8,128]{2,1,0:T(8,128)S(1)} custom-call(bf16[1152,128]{1,0:T(8,128)(2,1)S(1)} %all_gather.3.refs_0_, bf16[2304,128]{1,0:T(8,128)(2,1)S(1)} %bitcast.1, bf16[640,1792]{1,0:T(8,128)(2,1)} %constant.2.clone.refs_2_), custom_call_target="tpu_custom_call" | custom-call | flops 8000000000 | bytes 4000000 | tf_op jit(solution)/shard_map/similarity/pallas_call | solution.py:239
  50.1 15.4 %all_to_all.10.in_ref = f32[16,8,128]{2,1,0:T(8,128)S(1)} all-to-all(f32[16,8,128]{2,1,0:T(8,128)S(1)} %similarity.1), channel_id=1, replica_groups=mesh['row'=16,'col'=32] {'row'}, dimensions={0} | all-to-all | bytes 131072 | tf_op jit(solution)/shard_map/all_to_all | solution.py:274
  65.5 0.7 %assemble.1 = f32[3,1536]{1,0:T(4,128)} custom-call(f32[16,8,128]{2,1,0:T(8,128)S(1)} %all_to_all.10.in_ref), custom_call_target="tpu_custom_call" | custom-call | tf_op jit(solution)/shard_map/assemble/pallas_call | solution.py:276
Async XLA Ops:
  0.0 0.8 %copy-start = (f32[3,3,1024]{2,1,0:T(4,128)S(1)}, f32[3,3,1024]{2,1,0:T(4,128)}, u32[]{:S(2)}) copy-start(f32[3,3,1024]{2,1,0:T(4,128)} %x_ref.1) | copy-start | bytes 110596
  1.8 32.9 %all-to-all-start = ((bf16[32,72,128]{2,1,0:T(8,128)(2,1)}), bf16[32,72,128]{2,1,0:T(8,128)(2,1)S(1)}, u32[]{:S(2)}, u32[]{:S(2)}) async-start(bf16[32,72,128]{2,1,0:T(8,128)(2,1)} %get-tuple-element.8), calls=%async_computation | async-start | bytes 1179648 | tf_op jit(solution)/shard_map/all_to_all | solution.py:270

commit v3 on v2

--- a/solution.py
+++ b/solution.py
@@ -13,32 +13,27 @@
 LANES = 128
 
 
-def frequency_order(half_len):
-    quarter, whole = half_len // 2, half_len // 2 // LANES * LANES
-    even, odd = 2 * np.arange(quarter), 2 * np.arange(quarter) + 1
-    return np.concatenate([even[:whole], even[whole:], odd[whole:], odd[:whole]])
-
-
-def transform_tables(transform_len, half_lags):
+FINE = 32
+
+
+def transform_tables(samples, transform_len, half_lags):
     half_len = transform_len // 2
     step = 2.0 * math.pi / transform_len
-    order = frequency_order(half_len)
-    whole = half_len // 2 // LANES * LANES
-    rest = half_len // 2 - whole
-    sample = np.arange(half_len)[:, None]
-    angles = (sample * order[None, :]) % transform_len * step
-    real = np.cos(angles)
-    imag = np.where(order[None, :] == 0, np.where(sample % 2 == 0, 1.0, -1.0), -np.sin(angles))
-    evens, evens_rest = slice(0, whole), slice(whole, whole + rest)
-    odds_rest, odds = slice(whole + rest, half_len - whole), slice(half_len - whole, half_len)
-    forward = [real[:, evens], imag[:, evens], real[:, evens_rest], imag[:, evens_rest]]
-    forward += [real[:, odds], imag[:, odds], real[:, odds_rest], imag[:, odds_rest]]
+    freq = np.arange(half_len)
     lag = np.concatenate([np.arange(0, half_lags, 2), np.arange(1, half_lags, 2)])[None, :]
-    angles = (order[:, None] * lag) % transform_len * step
-    weight = np.where(order[:, None] == 0, 1.0, 2.0) / transform_len
-    cosine = weight * np.cos(angles)
-    sine = np.where(order[:, None] == 0, 0.0, -weight * np.sin(angles))
-    return np.concatenate([*forward, cosine, sine], axis=1).astype(np.float32).astype(jnp.bfloat16)
+    angles = (freq[:, None] * lag) % transform_len * step
+    weight = np.where(freq[:, None] == 0, 1.0, 2.0) / transform_len
+    inverse = np.zeros((half_len, half_len), np.float32)
+    inverse[:, :half_lags] = weight * np.cos(angles)
+    inverse[:, half_lags : 2 * half_lags] = np.where(freq[:, None] == 0, 0.0, -weight * np.sin(angles))
+    fine = (np.arange(FINE)[:, None] * freq) % transform_len * step
+    coarse = (FINE * np.arange(samples // FINE)[:, None] * freq) % transform_len * step
+    left = np.concatenate([np.cos(fine), np.sin(fine), np.cos(coarse), -np.sin(coarse)])
+    rows = [inverse.astype(jnp.bfloat16)]
+    for _ in range(3):
+        rows.append(left.astype(np.float32).astype(jnp.bfloat16))
+        left = left - rows[-1].astype(np.float64)
+    return np.concatenate(rows)
 
 
 def normalize_kernel(copies, x_ref, one_ref, many_ref, rows_ref):
@@ -73,7 +68,7 @@
 
 def similarity_kernel(comps, samples, chunk, step, *refs):
     (left_ref, right_ref, tables_hbm, out_ref,
-     basis_ref, even_ref, odd_ref, rows_ref, wave_ref,
+     part_ref, factor_ref, basis_ref, even_ref, odd_ref, rows_ref, wave_ref,
      l1_ref, l2_ref, l3_ref, r1_ref, r2_ref, r3_ref,
      ce0, co0, ce1, co1, me_ref, mo_ref, sems) = refs
     parts = samples // LANES
@@ -82,11 +77,10 @@
     half_len, lag_count = even_ref.shape
     tiles = half_len // LANES
 
-    width = 2 * half_len
-    sources = [slice(0, width), slice(width, width + lag_count), slice(width + lag_count, width + 2 * lag_count)]
     copies = [
-        pltpu.make_async_copy(tables_hbm.at[:, source], target, sems.at[k])
-        for k, (source, target) in enumerate(zip(sources, (basis_ref, even_ref, odd_ref)))
+        pltpu.make_async_copy(tables_hbm.at[half_len:, :], part_ref, sems.at[0]),
+        pltpu.make_async_copy(tables_hbm.at[:half_len, :lag_count], even_ref, sems.at[1]),
+        pltpu.make_async_copy(tables_hbm.at[:half_len, lag_count : 2 * lag_count], odd_ref, sems.at[2]),
     ]
     for copy in copies:
         copy.start()
@@ -115,45 +109,40 @@
         )
 
     copies[0].wait()
-    tail = samples - half_len
-
-    def product(cols):
-        low = jnp.dot(wave_ref[:, :half_len], basis_ref[:, cols], preferred_element_type=jnp.float32)
-        high = jnp.dot(wave_ref[:, half_len:], basis_ref[:tail, cols], preferred_element_type=jnp.float32)
-        return low, high
-
-    def rounded(values):
-        return values.astype(jnp.bfloat16).astype(jnp.float32)
-
-    low, high = product(slice(0, half_len))
-    evens = rounded(low + high)
-    low, high = product(slice(half_len, width))
-    odds = rounded(low - high)
-    whole = half_len // 2 // LANES
-    lane = lax.broadcasted_iota(jnp.int32, (1, LANES), 1)
-
-    def tile(values, k):
-        return values[:, k * LANES : (k + 1) * LANES]
-
-    def parts_of(f):
-        if f < whole:
-            return tile(evens, f), tile(evens, whole + f)
-        if f > whole:
-            return tile(odds, f - whole - 1), tile(odds, f - 1)
-        a, b = tile(evens, 2 * whole), tile(odds, 2 * whole)
-        half = LANES // 2
-        return (
-            jnp.where(lane < half, a, pltpu.roll(b, half, 1)),
-            jnp.where(lane < half, pltpu.roll(a, half, 1), b),
-        )
-
+    count = factor_ref.shape[0]
+    factor_ref[...] = (
+        part_ref[:count].astype(jnp.float32)
+        + part_ref[count : 2 * count].astype(jnp.float32)
+        + part_ref[2 * count :].astype(jnp.float32)
+    )
+    lane = lax.broadcasted_iota(jnp.int32, (FINE, LANES), 1)
+    row = lax.broadcasted_iota(jnp.int32, (FINE, LANES), 0)
+    alternate = jnp.where(lax.rem(row, 2) == 0, 1.0, -1.0)
+    for f in range(tiles):
+        fs = slice(f * LANES, (f + 1) * LANES)
+        cos_fine, sin_fine = factor_ref[:FINE, fs], factor_ref[FINE : 2 * FINE, fs]
+        for a in range(samples // FINE):
+            at = 2 * FINE + a
+            cos_coarse = factor_ref[at : at + 1, fs]
+            sin_coarse = factor_ref[at + samples // FINE : at + samples // FINE + 1, fs]
+            span = slice(a * FINE, (a + 1) * FINE)
+            basis_ref[span, fs] = (cos_coarse * cos_fine + sin_coarse * sin_fine).astype(jnp.bfloat16)
+            imag = sin_coarse * cos_fine - cos_coarse * sin_fine
+            if f == 0:
+                imag = jnp.where(lane == 0, alternate, imag)
+            basis_ref[span, half_len + f * LANES : half_len + (f + 1) * LANES] = imag.astype(jnp.bfloat16)
+
+    spectrum = jnp.dot(wave_ref[...], basis_ref[...], preferred_element_type=jnp.float32)
+    spectrum = spectrum.astype(jnp.bfloat16).astype(jnp.float32)
+    first = lax.broadcasted_iota(jnp.int32, (1, LANES), 1) == 0
     top = None
     for f in range(tiles):
         fs = slice(f * LANES, (f + 1) * LANES)
-        real, imag = parts_of(f)
+        real = spectrum[:, fs]
+        imag = spectrum[:, half_len + f * LANES : half_len + (f + 1) * LANES]
         if f == 0:
-            top = jnp.where(lane == 0, imag, 0.0).astype(jnp.bfloat16)
-            imag = jnp.where(lane == 0, 0.0, imag)
+            top = jnp.where(first, imag, 0.0).astype(jnp.bfloat16)
+            imag = jnp.where(first, 0.0, imag)
         l1_ref[f] = real[:split]
         l2_ref[f] = real[:split] - imag[:split]
         l3_ref[f] = real[:split] + imag[:split]
@@ -233,7 +222,8 @@
     parts = samples // LANES
     left = left_waves.shape[0] // (comps * parts)
     right = right_waves.shape[0] // (comps * parts)
-    tables = jnp.asarray(transform_tables(transform_len, LAGS // 2))
+    tables = jnp.asarray(transform_tables(samples, transform_len, LAGS // 2))
+    factors = 2 * (FINE + samples // FINE)
     chunk, step = 4, 32
     f32, bf16 = jnp.float32, jnp.bfloat16
     return pl.pallas_call(
@@ -241,7 +231,9 @@
         out_shape=jax.ShapeDtypeStruct((owners, 8, LANES), f32),
         in_specs=[pl.BlockSpec(memory_space=pltpu.VMEM)] * 2 + [pl.BlockSpec(memory_space=pltpu.HBM)],
         scratch_shapes=[
-            pltpu.VMEM((half_len, transform_len), bf16),
+            pltpu.VMEM((3 * factors, half_len), bf16),
+            pltpu.VMEM((factors, half_len), f32),
+            pltpu.VMEM((samples, transform_len), bf16),
             *[pltpu.VMEM((half_len, LAGS // 2), bf16)] * 2,
             pltpu.VMEM((right * comps * parts, LANES), f32),
             pltpu.VMEM(((left + right) * comps, samples), bf16),
@@ -251,7 +243,7 @@
             *[pltpu.VMEM((right, left), f32)] * 2,
             pltpu.SemaphoreType.DMA((3,)),
         ],
-        compiler_params=pltpu.CompilerParams(vmem_limit_bytes=54_500_000),
+        compiler_params=pltpu.CompilerParams(vmem_limit_bytes=55_000_000),
         cost_estimate=pl.CostEstimate(flops=8_000_000_000, bytes_accessed=4_000_000, transcendentals=0),
         name="similarity",
     )(left_waves, right_waves, tables)

time: 66.5 us -> 66.1 us (level)
  no operation moved by 1% of the time
where the time goes in v3:
time: 66.1 us; the launch traced here: 65.8 us
  blocking collectives  34.6 us (52%)
  Pallas kernels  16.6 us (25%)
  starting transfers between devices  13.7 us (21%)
  local copies, waits for them, and re-layouts  0.8 us (1%)
    all_gather x1, blocking collectives, body(): owned = lax.all_gather(one, 'row', tiled=True)  19.2 us
    all_to_all x1, blocking collectives, body(): mine = lax.all_to_all(block, 'row', split_axis=0, concat_axis=0, tiled=True)  15.4 us
    pallas_call x1, Pallas kernels, similarity(): pl.pallas_call(functools.partial(similarity_kernel, comps, samples, chunk...  15 us
    all_to_all x1, starting transfers between devices, body(): lax.all_to_all(many, 'col', split_axis=0, concat_axis=0, tiled=True)  13.7 us
  transfers between devices with their start and end apart: 1, of which 0 were waited for; matrix products, arithmetic and copies ran while one was open for 0% of the time, Pallas kernels for 0%

profile of v3, /device:TPU:1, one launch (start us, length us, event | category | flops | bytes accessed | tf_op | source)
XLA Modules:
  0.0 65.8 jit_solution(8493257039885001706)
XLA Ops:
  0.0 0.0 copy-start
  0.0 0.8 %copy-done = f32[3,3,1024]{2,1,0:T(4,128)S(1)} copy-done((f32[3,3,1024]{2,1,0:T(4,128)S(1)}, f32[3,3,1024]{2,1,0:T(4,128)}, u32[]{:S(2)}) %copy-start) | copy-done | bytes 36888
  0.8 1.0 %normalize.1 = (bf16[72,128]{1,0:T(8,128)(2,1)S(1)}, bf16[32,72,128]{2,1,0:T(8,128)(2,1)}) custom-call(f32[3,3,1024]{2,1,0:T(4,128)S(1)} %copy-done), custom_call_target="tpu_custom_call" | custom-call | tf_op jit(solution)/shard_map/normalize/pallas_call | solution.py:57
  1.8 13.7 %all-to-all-start = ((bf16[32,72,128]{2,1,0:T(8,128)(2,1)}), bf16[32,72,128]{2,1,0:T(8,128)(2,1)S(1)}, u32[]{:S(2)}, u32[]{:S(2)}) async-start(bf16[32,72,128]{2,1,0:T(8,128)(2,1)} %get-tuple-element.8), calls=%async_computation | async-start | bytes 1179648 | tf_op jit(solution)/shard_map/all_to_all | solution.py:262
  15.5 19.2 %all_gather.3.refs_0_ = bf16[1152,128]{1,0:T(8,128)(2,1)S(1)} all-gather(bf16[72,128]{1,0:T(8,128)(2,1)S(1)} %get-tuple-element.7), channel_id=1, replica_groups=mesh['row'=16,'col'=32] {'row'}, dimensions={0}, use_global_device_ids=true | all-gather | bytes 313344 | tf_op jit(solution)/shard_map/all_gather | solution.py:263
  34.7 0.0 all-to-all-done
  34.7 15.0 %similarity.1 = f32[16,8,128]{2,1,0:T(8,128)S(1)} custom-call(bf16[1152,128]{1,0:T(8,128)(2,1)S(1)} %all_gather.3.refs_0_, bf16[2304,128]{1,0:T(8,128)(2,1)S(1)} %bitcast.1, bf16[1024,640]{1,0:T(8,128)(2,1)} %constant.2.clone.refs_2_), custom_call_target="tpu_custom_call" | custom-call | flops 8000000000 | bytes 4000000 | tf_op jit(solution)/shard_map/similarity/pallas_call | solution.py:229
  49.7 15.4 %all_to_all.10.in_ref = f32[16,8,128]{2,1,0:T(8,128)S(1)} all-to-all(f32[16,8,128]{2,1,0:T(8,128)S(1)} %similarity.1), channel_id=1, replica_groups=mesh['row'=16,'col'=32] {'row'}, dimensions={0} | all-to-all | bytes 131072 | tf_op jit(solution)/shard_map/all_to_all | solution.py:266
  65.1 0.7 %assemble.1 = f32[3,1536]{1,0:T(4,128)} custom-call(f32[16,8,128]{2,1,0:T(8,128)S(1)} %all_to_all.10.in_ref), custom_call_target="tpu_custom_call" | custom-call | tf_op jit(solution)/shard_map/assemble/pallas_call | solution.py:268
Async XLA Ops:
  0.0 0.8 %copy-start = (f32[3,3,1024]{2,1,0:T(4,128)S(1)}, f32[3,3,1024]{2,1,0:T(4,128)}, u32[]{:S(2)}) copy-start(f32[3,3,1024]{2,1,0:T(4,128)} %x_ref.1) | copy-start | bytes 110596
  1.8 32.9 %all-to-all-start = ((bf16[32,72,128]{2,1,0:T(8,128)(2,1)}), bf16[32,72,128]{2,1,0:T(8,128)(2,1)S(1)}, u32[]{:S(2)}, u32[]{:S(2)}) async-start(bf16[32,72,128]{2,1,0:T(8,128)(2,1)} %get-tuple-element.8), calls=%async_computation | async-start | bytes 1179648 | tf_op jit(solution)/shard_map/all_to_all | solution.py:262
